TPU v7x, 16 devices: a 4x2x1 block of a 4x4x8 slice. The times are simulated.
16 devices in a mesh: dp: 2 (over y, z), ctx: 8 (over x, core).
Axes of the slice: x: 4, y: 2, z: 1, core: 2. Of those that a mesh axis runs over, the one named last changes fastest.
The devices are a block of a 4x4x8 slice.
Arguments:
- hidden: bfloat16 [512, 2048], P(('dp', 'ctx')), parts along dimension 0
- w_q: bfloat16 [2048, 3072], replicated
- w_uk: bfloat16 [16, 128, 512], replicated
- w_uv: bfloat16 [16, 512, 128], replicated
- w_o: bfloat16 [2048, 2048], replicated
- kv_prefix: bfloat16 [32768, 576], P(('dp', 'ctx')), parts along dimension 0
- kv_suffix: bfloat16 [512, 2048, 576], P(('dp', 'ctx')), parts along dimension 0
- seq_lens: int32 [512], P(('dp', 'ctx')), parts along dimension 0
Outputs:
- output: bfloat16 [512, 2048], P(('dp', 'ctx')), parts along dimension 0
There are 2 independent parts. A program takes and returns all parts, laid end to end along the dimension named above; an argument that names none is the same for every part.
All inputs are finite; a program needn't handle non-finite values.
Results may differ from a plain program's by a relative error of at most 0.00657954.
Values are sent between devices in bfloat16 or wider.
A program may use at most 768 MiB of HBM per device.

v0:
```python
import functools
import math
import jax
import jax.numpy as jnp
from jax import lax
from jax.experimental import pallas as pl
from jax.experimental.pallas import tpu as pltpu
from jax.sharding import PartitionSpec as P

ROPE_BASE = 10000
LOG2E = math.log2(math.e)
CORES = 2
F32 = jnp.float32
BF16 = jnp.bfloat16
HBM = pl.BlockSpec(memory_space=pltpu.HBM)
VMEM = pl.BlockSpec(memory_space=pltpu.VMEM)
SMEM = pl.BlockSpec(memory_space=pltpu.SMEM)
NT = (((1,), (1,)), ((), ()))


def rope_table(positions, half_dim):
    lane = jnp.arange(4 * half_dim)
    inv_freq = jnp.exp((lane % half_dim).astype(F32) * (-math.log(ROPE_BASE) / half_dim))
    angle = positions.astype(F32)[:, None] * inv_freq
    return jnp.where(lane < 2 * half_dim, jnp.cos(angle), jnp.sin(angle))


def prefix_part(scale2, lat, q_ref, k_ref, outs, work, hook=None, loaded=False, next_ref=None):
    s_ref, p_ref, acc_ref, a_ref, m_ref, l_ref = work
    rows, sub = q_ref.shape[0], s_ref.shape[2]
    count = k_ref.shape[1] // sub
    chunk = 64
    m_ref[...] = jnp.full_like(m_ref, -jnp.inf)
    l_ref[...] = jnp.zeros_like(l_ref)
    acc_ref[...] = jnp.zeros_like(acc_ref)

    def keys(n):
        return pl.ds(pl.multiple_of(n * sub, sub), sub)

    def scores(n, slot, ref=q_ref):
        s_ref[slot] = jnp.dot(ref[...], k_ref[:, keys(n)], preferred_element_type=F32)

    def absorb(n, slot):
        for r in range(0, rows, chunk):
            cut = slice(r, r + chunk)
            s = s_ref[slot, cut, :]
            m_old = m_ref[cut, :]
            m_new = jnp.maximum(m_old, jnp.max(s, axis=1, keepdims=True) * scale2)
            alpha = jnp.exp2(m_old - m_new)
            l_new = l_ref[cut, :] * alpha
            for k in range(0, sub, 128):
                p = jnp.exp2(s[:, k:k + 128] * scale2 - m_new)
                l_new = l_new + p
                p_ref[slot, cut, k:k + 128] = p.astype(BF16)
            l_ref[cut, :] = l_new
            m_ref[cut, :] = m_new
            a_ref[cut, :] = alpha
        pv = lax.dot_general(p_ref[slot], k_ref[0:lat, keys(n)], NT, preferred_element_type=F32)
        alpha = a_ref[...]
        for k in range(0, lat, 128):
            acc_ref[:, k:k + 128] = acc_ref[:, k:k + 128] * alpha + pv[:, k:k + 128]

    if not loaded:
        scores(0, 0)
    if hook is not None:
        hook()

    def pair(i, carry):
        scores(2 * i + 1, 1)
        absorb(2 * i, 0)
        scores(2 * i + 2, 0)
        absorb(2 * i + 1, 1)
        return carry

    lax.fori_loop(0, count // 2 - 1, pair, 0)
    scores(count - 1, 1)
    absorb(count - 2, 0)
    if next_ref is not None:
        scores(0, 0, next_ref)
    absorb(count - 1, 1)
    m_t = m_ref[...].T[0:1]
    l_t = jnp.broadcast_to(jnp.sum(l_ref[...], axis=1, keepdims=True), (rows, 128)).T[0:1]
    size = rows // len(outs)
    for k, ref in enumerate(outs):
        cut = slice(k * size, (k + 1) * size)
        ref[0:size, :] = acc_ref[cut, :]
        ref[size:size + 1, 0:size] = m_t[:, cut]
        ref[size + 1:size + 2, 0:size] = l_t[:, cut]


def merge_into(x_ref, y_ref, offset):
    rows, half = x_ref.shape[0] - 8, y_ref.shape[0] - 8
    cut = slice(offset, offset + half)
    m_x, m_y = x_ref[rows:rows + 1, cut], y_ref[half:half + 1, 0:half]
    l_x, l_y = x_ref[rows + 1:rows + 2, cut], y_ref[half + 1:half + 2, 0:half]
    m_all = jnp.maximum(m_x, m_y)
    w_x, w_y = jnp.exp2(m_x - m_all), jnp.exp2(m_y - m_all)
    x_ref[rows:rows + 1, cut] = m_all
    x_ref[rows + 1:rows + 2, cut] = l_x * w_x + l_y * w_y
    c_x = jnp.broadcast_to(w_x, (8, half)).T[:, 0:1]
    c_y = jnp.broadcast_to(w_y, (8, half)).T[:, 0:1]
    x_ref[cut, :] = x_ref[cut, :] * c_x + y_ref[0:half, :] * c_y


def prefix_kernel(chips, scale2, hid_ref, cs_ref, wq_hbm, wuk_hbm, kv_hbm, q_out, own_out, up_out, down_out,
                  hid_all, cs_all, wq_buf, wuk_buf, k_ref, q_buf, res, far, got,
                  s_ref, p_ref, acc_ref, a_ref, m_ref, l_ref,
                  wq_sem, wuk_sem, kv_sem, out_sem, hid_send, hid_recv, cs_send, cs_recv, kv_send, kv_recv, far_send, far_recv):
    me = lax.axis_index('ctx')
    chip, core = me // CORES, me % CORES
    steps, _, wide = wq_buf.shape
    rows = hid_ref.shape[0]
    heads, nope, lat = wuk_buf.shape
    rope = q_buf.shape[2] - lat
    head_w = nope + rope
    keys = kv_hbm.shape[1]
    per = wide // head_w
    work = (s_ref, p_ref, acc_ref, a_ref, m_ref, l_ref)

    def weight_copy(i):
        return pltpu.make_async_copy(wq_hbm.at[:, pl.ds(i * wide, wide)], wq_buf.at[i], wq_sem.at[i])

    def remote(src, dst, send, recv, dev):
        return pltpu.make_async_remote_copy(src, dst, send, recv, device_id={'ctx': dev}, device_id_type=pl.DeviceIdType.MESH)

    weight_copy(0).start()
    uk_copy = pltpu.make_async_copy(wuk_hbm, wuk_buf, wuk_sem)
    uk_copy.start()
    for i in range(1, steps):
        weight_copy(i).start()
    own_copy = pltpu.make_async_copy(kv_hbm, k_ref.at[:, pl.ds(0, keys)], kv_sem)
    own_copy.start()
    partner = chip * CORES + (1 - core)
    peers = [((chip + chips - r) % chips) * CORES + core for r in range(1, chips)]
    barrier = pltpu.get_barrier_semaphore()
    for dev in [partner] + peers:
        pl.semaphore_signal(barrier, inc=1, device_id={'ctx': dev}, device_id_type=pl.DeviceIdType.MESH)
    pl.semaphore_wait(barrier, chips)
    copies = []
    for r in range(1, chips):
        copies.append(remote(hid_ref, hid_all.at[r - 1], hid_send.at[r - 1], hid_recv.at[r - 1], peers[r - 1]))
        copies.append(remote(cs_ref, cs_all.at[r - 1], cs_send.at[r - 1], cs_recv.at[r - 1], peers[r - 1]))
    kv_copy = remote(kv_hbm, k_ref.at[:, pl.ds(keys, keys)], kv_send, kv_recv, partner)
    kv_copy.start()
    for c in copies:
        c.start()

    def queries(x, cs, first, own):
        cos, sin = cs[:, :rope], cs[:, rope:]
        for i in range(steps):
            if own:
                weight_copy(i).wait()
            qa = jnp.dot(x, wq_buf[i], preferred_element_type=F32).astype(BF16)
            if own and i == 0:
                uk_copy.wait()
            for k in range(per):
                h = i * per + k
                q_lat = jnp.dot(qa[:, k * head_w:k * head_w + nope], wuk_buf[h], preferred_element_type=F32).astype(BF16)
                pe = qa[:, k * head_w + nope:(k + 1) * head_w].astype(F32)
                turned = jnp.concatenate([-pe[:, rope // 2:], pe[:, :rope // 2]], axis=1)
                pe = (pe * cos + turned * sin).astype(BF16)
                for r in range(x.shape[0] // rows):
                    q_buf[first + r, h * rows:(h + 1) * rows, 0:lat] = q_lat[r * rows:(r + 1) * rows]
                    q_buf[first + r, h * rows:(h + 1) * rows, lat:lat + rope] = pe[r * rows:(r + 1) * rows]

    queries(hid_ref[...], cs_ref[...], 0, True)
    q_copy = pltpu.make_async_copy(q_buf.at[0], q_out, out_sem.at[0])
    own_copy.wait()
    kv_copy.wait()
    prefix_part(scale2, lat, q_buf.at[0], k_ref, [res.at[0]], work, q_copy.start)
    for c in copies:
        c.wait()
    queries(hid_all[...].reshape((chips - 1) * rows, hid_ref.shape[1]), cs_all[...].reshape((chips - 1) * rows, 2 * rope), 1, False)
    own_done = pltpu.make_async_copy(res.at[0], own_out, out_sem.at[1])
    prefix_part(scale2, lat, q_buf.at[2], k_ref, [far.at[0], far.at[1]], work, own_done.start, next_ref=q_buf.at[1])
    sends = [remote(far.at[n], got.at[n], far_send.at[n], far_recv.at[n], dev) for n, dev in enumerate((peers[2], peers[0]))]

    def send_far():
        for c in sends:
            c.start()

    prefix_part(scale2, lat, q_buf.at[1], k_ref, [res.at[1]], work, send_far, loaded=True, next_ref=q_buf.at[3])
    prefix_part(scale2, lat, q_buf.at[3], k_ref, [res.at[2]], work, loaded=True)
    for c in sends:
        c.wait()
    merge_into(res.at[1], got.at[0], 0)
    merge_into(res.at[2], got.at[1], heads * rows // 2)
    last = [pltpu.make_async_copy(res.at[1], up_out, out_sem.at[2]), pltpu.make_async_copy(res.at[2], down_out, out_sem.at[3])]
    for c in last:
        c.start()
    for c in [q_copy, own_done] + last:
        c.wait()


def prefix_parts(hidden, cs, w_q, w_uk, kv_prefix, scale2, chips):
    rows, depth = hidden.shape
    heads, nope, lat = w_uk.shape
    rope = w_q.shape[1] // heads - nope
    steps, sub = 4, 1024
    wide = w_q.shape[1] // steps
    flat = heads * rows
    keys = CORES * kv_prefix.shape[1]
    others = chips - 1
    full, half = (flat + 8, lat), (flat // 2 + 8, lat)
    dma = pltpu.SemaphoreType.DMA
    return pl.pallas_call(
        functools.partial(prefix_kernel, chips, scale2),
        out_shape=[jax.ShapeDtypeStruct((flat, lat + rope), BF16)] + [jax.ShapeDtypeStruct(full, F32)] * 3,
        in_specs=[VMEM, VMEM, HBM, HBM, HBM],
        out_specs=[HBM] * 4,
        scratch_shapes=[
            pltpu.VMEM((others, rows, depth), BF16), pltpu.VMEM((others, rows, 2 * rope), F32),
            pltpu.VMEM((steps, depth, wide), BF16), pltpu.VMEM(w_uk.shape, BF16),
            pltpu.VMEM((kv_prefix.shape[0], keys), BF16), pltpu.VMEM((chips, flat, lat + rope), BF16),
            pltpu.VMEM((3,) + full, F32), pltpu.VMEM((2,) + half, F32), pltpu.VMEM((2,) + half, F32),
            pltpu.VMEM((2, flat, sub), F32), pltpu.VMEM((2, flat, sub), BF16), pltpu.VMEM((flat, lat), F32)]
            + [pltpu.VMEM((flat, 128), F32)] * 3
            + [dma((steps,)), dma, dma, dma((4,)), dma((others,)), dma((others,)), dma((others,)), dma((others,)), dma, dma, dma((2,)), dma((2,))],
        compiler_params=pltpu.CompilerParams(collective_id=0, has_side_effects=True, vmem_limit_bytes=60 * 2**20),
        cost_estimate=pl.CostEstimate(flops=2 * chips * flat * keys * (768 + lat), bytes_accessed=2 * w_q.size, transcendentals=chips * flat * keys),
        name='prefix',
    )(hidden, cs, w_q, w_uk, kv_prefix)


def suffix_kernel(scale2, lat, heads, unroll, lens_ref, q_ref, kv_hbm, o_ref, m_out, l_out, q_buf, acc_ref, bufs, sems):
    seqs = q_ref.shape[0] // heads
    width = q_ref.shape[1]
    depth, size = bufs.shape[0], bufs.shape[2]
    lanes = [(k, min(k + 128, width)) for k in range(0, width, 128)]

    total = lax.fori_loop(0, seqs, lambda b, n: n + lens_ref[b] // size + 1, 0)

    def advance(b, j):
        last = j >= lens_ref[jnp.minimum(b, seqs - 1)] // size
        return jnp.where(last, b + 1, b), jnp.where(last, 0, j + 1)

    def rows_of(b):
        return pl.ds(jnp.minimum(b, seqs - 1), heads, stride=seqs)

    def copy(b, j, slot):
        return pltpu.make_async_copy(kv_hbm.at[b, :, pl.ds(pl.multiple_of(j * size, size), size)], bufs.at[slot], sems.at[slot])

    def scores(b, slot):
        q = jnp.concatenate([q_buf[n, rows_of(b), :][:, 0:hi - lo] for n, (lo, hi) in enumerate(lanes)], axis=1).astype(BF16)
        return jnp.dot(q, bufs[slot], preferred_element_type=F32)

    zero = jnp.int32(0)
    items = [(zero, zero)]
    for n in range(depth - unroll):
        copy(*items[n], n).start()
        items.append(advance(*items[n]))
    for n, (lo, hi) in enumerate(lanes):
        q_buf[n, :, 0:hi - lo] = q_ref[:, lo:hi].astype(F32)
    acc_ref[...] = jnp.zeros_like(acc_ref)
    for n in range(unroll):
        copy(*items[n], n).wait()
    pos = lax.broadcasted_iota(jnp.int32, (heads, size), 1)

    def flush(b, n):
        for k in range(lat // 128):
            o_ref[k, rows_of(b), :] = acc_ref[n, :, k * 128:(k + 1) * 128]

    def absorb(b, j, slot, s, m, l, before, n):
        live = b < seqs
        limit = jnp.where(live, lens_ref[jnp.minimum(b, seqs - 1)] - j * size, -1)
        s2 = jnp.where(pos <= limit, s * scale2, -jnp.inf)
        m_old = jnp.where(jnp.logical_and(live, j == 0), -jnp.inf, m)
        m_new = jnp.maximum(m_old, jnp.max(s2, axis=1, keepdims=True))
        alpha = jnp.exp2(m_old - m_new)
        p = [jnp.exp2(s2[:, k:k + 128] - m_new) for k in range(0, size, 128)]
        l_new = l * alpha + functools.reduce(jnp.add, p)
        p = jnp.concatenate([x.astype(BF16) for x in p], axis=1)
        pv = lax.dot_general(p, bufs[slot, 0:lat, :], NT, preferred_element_type=F32)
        for k in range(0, lat, 128):
            acc_ref[n, :, k:k + 128] = acc_ref[before, :, k:k + 128] * alpha + pv[:, k:k + 128]
        m_out[rows_of(b), :] = m_new
        l_out[rows_of(b), :] = l_new
        return m_new, l_new

    def body(i, carry):
        prev, now, later, fetching, s_now, m, l = carry
        t = unroll * i
        for n in range(unroll):
            @pl.when(t + depth - unroll + n < total)
            def _():
                copy(*fetching, lax.rem(t + depth - unroll + n, depth)).start()
            fetching = advance(*fetching)
        for n in range(unroll):
            @pl.when(t + unroll + n < total)
            def _():
                copy(*later[n], lax.rem(t + unroll + n, depth)).wait()
        for n in range(unroll):
            flush(prev[n], n)
        s_next = [scores(later[n][0], lax.rem(t + unroll + n, depth)) for n in range(unroll)]
        for n in range(unroll):
            m, l = absorb(*now[n], lax.rem(t + n, depth), s_now[n], m, l, (n - 1) % unroll, n)
        coming = [advance(*later[-1])]
        for n in range(1, unroll):
            coming.append(advance(*coming[-1]))
        return [b for b, _ in now], later, coming, fetching, s_next, m, l

    later = items[unroll:2 * unroll]
    s_now = [scores(items[n][0], n) for n in range(unroll)]
    stat = jnp.zeros((heads, 128), F32)
    first = [items[0][0]] * unroll
    carry = (first, items[:unroll], later, items[-1], s_now, stat, stat)
    carry = lax.fori_loop(0, (total + unroll - 1) // unroll, body, carry)
    for n in range(unroll):
        flush(carry[0][n], n)


def suffix_part(q_rows, kv_suffix, seq_lens, heads, scale2, lat):
    rows, width = q_rows.shape
    seqs, _, slots = kv_suffix.shape
    size, depth, unroll = 512, 16, 4
    stat = jax.ShapeDtypeStruct((rows, 128), F32)
    return pl.pallas_call(
        functools.partial(suffix_kernel, scale2, lat, heads, unroll),
        out_shape=[jax.ShapeDtypeStruct((lat // 128, rows, 128), F32), stat, stat],
        in_specs=[SMEM, VMEM, HBM],
        out_specs=[VMEM, VMEM, VMEM],
        scratch_shapes=[pltpu.VMEM((-(-width // 128), rows, 128), F32), pltpu.VMEM((unroll, heads, lat), F32), pltpu.VMEM((depth, width, size), BF16), pltpu.SemaphoreType.DMA((depth,))],
        compiler_params=pltpu.CompilerParams(vmem_limit_bytes=32 * 2**20),
        cost_estimate=pl.CostEstimate(flops=2 * seqs * slots * 256 * 768, bytes_accessed=seqs * slots * width * 2, transcendentals=seqs * slots * heads),
        name='suffix',
    )(seq_lens, q_rows, kv_suffix)


def stats_of(ref, size):
    both = ref[size:size + 8, 0:size].T
    return both[:, 0:1], both[:, 1:2]


def output_kernel(hid_ref, os_ref, ms_ref, ls_ref, *refs):
    parts, (uv_ref, wo_ref, out_ref, v_buf) = refs[:3], refs[3:]
    rows, heads = hid_ref.shape[0], uv_ref.shape[0]
    lat, width = uv_ref.shape[1], uv_ref.shape[2]
    flat = rows * heads
    stats = [stats_of(ref, flat) for ref in parts]
    for h in range(heads):
        cut = slice(h * rows, (h + 1) * rows)
        m_s, l_s = ms_ref[cut, 0:1], jnp.sum(ls_ref[cut, :], axis=1, keepdims=True)
        ms = [m_s] + [m[cut] for m, _ in stats]
        ls = [l_s] + [l[cut] for _, l in stats]
        m_all = functools.reduce(jnp.maximum, ms)
        ws = [jnp.exp2(m - m_all) for m in ms]
        l_all = functools.reduce(jnp.add, [l * w for l, w in zip(ls, ws)])
        o_s = jnp.concatenate([os_ref[n, cut, :] for n in range(lat // 128)], axis=1)
        o_all = o_s * ws[0]
        for ref, w in zip(parts, ws[1:]):
            o_all = o_all + ref[cut, :] * w
        o_h = (o_all / l_all).astype(BF16)
        v_buf[:, h * width:(h + 1) * width] = jnp.dot(o_h, uv_ref[h], preferred_element_type=F32).astype(BF16)
    proj = jnp.dot(v_buf[...], wo_ref[...], preferred_element_type=F32)
    out_ref[...] = (hid_ref[...].astype(F32) + proj).astype(BF16)


def output_part(hidden, suffix, parts, w_uv, w_o):
    rows = hidden.shape[0]
    heads, lat, val = w_uv.shape
    return pl.pallas_call(
        output_kernel,
        out_shape=jax.ShapeDtypeStruct(hidden.shape, BF16),
        in_specs=[VMEM] * 9,
        out_specs=VMEM,
        scratch_shapes=[pltpu.VMEM((rows, heads * val), BF16)],
        compiler_params=pltpu.CompilerParams(vmem_limit_bytes=24 * 2**20),
        cost_estimate=pl.CostEstimate(flops=2 * rows * heads * val * (lat + hidden.shape[1]), bytes_accessed=2 * (w_uv.size + w_o.size), transcendentals=0),
        name='output',
    )(hidden, *suffix, *parts, w_uv, w_o)


def solution(mesh):
    group = mesh.shape['ctx']
    chips = group // CORES
    rows_spec = P(('dp', 'ctx'), None)
    whole_spec = P()

    def local_step(hidden, w_q, w_uk, w_uv, w_o, kv_prefix, kv_suffix, seq_lens):
        rows = hidden.shape[0]
        heads, nope, lat = w_uk.shape
        head_w = w_q.shape[1] // heads
        rope = head_w - nope
        prefix_len = kv_prefix.shape[0] * group
        scale2 = head_w ** -0.5 * LOG2E
        kv_prefix = kv_prefix.T
        kv_suffix = kv_suffix.transpose(0, 2, 1)
        cs = rope_table(prefix_len + seq_lens, rope // 2)
        query, own, up, down = prefix_parts(hidden, cs, w_q, w_uk, kv_prefix, scale2, chips)

        def send(value, hop):
            return lax.ppermute(value, 'ctx', [(j, (j + hop * CORES) % group) for j in range(group)])

        in_up, in_down = send(up, 1), send(down, -1)
        suffix = suffix_part(query, kv_suffix, seq_lens, heads, scale2, lat)
        return output_part(hidden, suffix, (own, in_up, in_down), w_uv, w_o)

    return jax.shard_map(local_step, mesh=mesh, in_specs=(rows_spec, whole_spec, whole_spec, whole_spec, whole_spec, rows_spec, P(('dp', 'ctx'), None, None), P(('dp', 'ctx'))), out_specs=rows_spec, check_vma=False)
```

profile of v0, /device:TPU:112, one launch (start us, length us, event | category | flops | bytes accessed | tf_op | source)
XLA Modules:
  0.0 82.2 jit_solution(11840088094447770382)
XLA Ops:
  0.0 0.7 add_convert_fusion
  0.7 0.8 fusion.cs_ref
  1.4 0.0 copy-start.3
  1.4 44.5 %prefix.1 = (bf16[512,576]{1,0:T(8,128)(2,1)}, f32[520,512]{1,0:T(8,128)}, f32[520,512]{1,0:T(8,128)}, f32[520,512]{1,0:T(8,128)}) custom-call(bf16[32,2048]{1,0:T(8,128)(2,1)} %hid_ref.3, f32[32,128]{1,0:T(8,128)} %fusion.cs_ref, bf16[2048,3072]{1,0:T(8,128)(2,1)} %wq_hbm.1, bf16[16,128,512]{2,1,0:T(8,128)(2,1)} %wuk_hbm.1, bf16[576,2048]{1,0:T(8,128)(2,1)} %bitcast.4), custom_call_target="tpu_custom_call" | custom-call | flops 21474836480 | bytes 12582912 | tf_op jit(solution)/shard_map/prefix/pallas_call | solution.py:206
  45.9 0.2 collective-permute-start
  46.1 3.1 %collective-permute-start.1 = (f32[520,512]{1,0:T(8,128)}, f32[520,512]{1,0:T(8,128)S(1)}, u32[]{:S(2)}, u32[]{:S(2)}) collective-permute-start(f32[520,512]{1,0:T(8,128)} %get-tuple-element.18), channel_id=1, source_target_pairs={{0,6},{1,7},{2,0},{3,1},{4,2},{5,3},{6,4},{7,5},{8,14},{9,15},{10,... | collective-permute-start | bytes 3194888 | tf_op jit(solution)/shard_map/ppermute | solution.py:392
  49.2 0.0 slice-start
  49.2 0.0 copy-done.3
  49.2 0.0 copy-start.4
  49.2 1.2 %copy-done.4 = bf16[512,576]{1,0:T(8,128)(2,1)S(1)} copy-done((bf16[512,576]{1,0:T(8,128)(2,1)S(1)}, bf16[512,576]{1,0:T(8,128)(2,1)}, u32[]{:S(2)}) %copy-start.4) | copy-done | bytes 589848
  50.5 0.0 slice-start.1
  50.5 0.0 copy-start
  50.5 0.0 copy-start.1
  50.5 0.0 copy-start.2
  50.5 27.4 %suffix.1 = (f32[4,512,128]{2,1,0:T(8,128)S(1)}, f32[512,128]{1,0:T(8,128)S(1)}, f32[512,128]{1,0:T(8,128)S(1)}) custom-call(s32[32]{0:T(128)S(1)} %copy-done.3, bf16[512,576]{1,0:T(8,128)(2,1)S(1)} %copy-done.4, bf16[32,576,2048]{2,1,0:T(8,128)(2,1)} %bitcast.1.kv_hbm), custom_call_target="tpu_custom_call" | custom-call | flops 25769803776 | bytes 75497472 | tf_op jit(solution)/shard_map/suffix/pallas_call | solution.py:317
  77.9 0.0 collective-permute-done.refs_1_
  77.9 0.0 collective-permute-done.1.refs_2_
  77.9 0.0 slice-done
  77.9 0.0 slice-done.1
  77.9 0.0 copy-done
  77.9 0.0 copy-done.1
  77.9 0.0 copy-done.2
  78.0 4.3 %output.1 = bf16[32,2048]{1,0:T(8,128)(2,1)} custom-call(bf16[32,2048]{1,0:T(8,128)(2,1)S(1)} %copy-done.2, f32[4,512,128]{2,1,0:T(8,128)S(1)} %get-tuple-element.13.os_ref, f32[512,128]{1,0:T(8,128)S(1)} %get-tuple-element.14.ms_ref, f32[512,128]{1,0:T(8,128)S(1)} %get-tuple-element.15.ls_ref, f32[520,512]{1,0:T(8,128)S(1)} %copy-done.1, ...), custom_call_target="tpu_custom_call" | custom-call | flops 335544320 | bytes 10485760 | tf_op jit(solution)/shard_map/output/pallas_call | solution.py:361
  (3 shorter events, 0.0 us)
Async XLA Ops:
  1.4 47.8 %copy-start.3 = (s32[32]{0:T(128)S(1)}, s32[32]{0:T(128)}, u32[]{:S(2)}) copy-start(s32[32]{0:T(128)} %lens_ref.1) | copy-start | bytes 388
  45.9 32.0 %collective-permute-start = (f32[520,512]{1,0:T(8,128)}, f32[520,512]{1,0:T(8,128)S(1)}, u32[]{:S(2)}, u32[]{:S(2)}) collective-permute-start(f32[520,512]{1,0:T(8,128)} %get-tuple-element.17), channel_id=1, source_target_pairs={{0,2},{1,3},{2,4},{3,5},{4,6},{5,7},{6,0},{7,1},{8,10},{9,11},{10,... | collective-permute-start | bytes 3194888 | tf_op jit(solution)/shard_map/ppermute | solution.py:392
  46.1 31.8 %collective-permute-start.1 = (f32[520,512]{1,0:T(8,128)}, f32[520,512]{1,0:T(8,128)S(1)}, u32[]{:S(2)}, u32[]{:S(2)}) collective-permute-start(f32[520,512]{1,0:T(8,128)} %get-tuple-element.18), channel_id=1, source_target_pairs={{0,6},{1,7},{2,0},{3,1},{4,2},{5,3},{6,4},{7,5},{8,14},{9,15},{10,... | collective-permute-start | bytes 3194888 | tf_op jit(solution)/shard_map/ppermute | solution.py:392
  49.2 28.7 %slice-start = ((s8[8388608]{0:T(1024)(128)(4,1)}), s8[4194304]{0:T(1024)(128)(4,1)S(1)}, s32[]{:S(2)}) async-start(s8[8388608]{0:T(1024)(128)(4,1)} %bitcast.2), calls=%async_computation | async-start | bytes 8388608
  49.2 1.2 %copy-start.4 = (bf16[512,576]{1,0:T(8,128)(2,1)S(1)}, bf16[512,576]{1,0:T(8,128)(2,1)}, u32[]{:S(2)}) copy-start(bf16[512,576]{1,0:T(8,128)(2,1)} %get-tuple-element.12.q_ref) | copy-start | bytes 1769476
  50.5 27.4 %slice-start.1 = ((s8[8388608]{0:T(1024)(128)(4,1)}), s8[4194304]{0:T(1024)(128)(4,1)S(1)}, s32[]{:S(2)}) async-start(s8[8388608]{0:T(1024)(128)(4,1)} %bitcast.2), calls=%async_computation.1 | async-start | bytes 8388608
  50.5 27.4 %copy-start = (bf16[16,512,128]{2,1,0:T(8,128)(2,1)S(1)}, bf16[16,512,128]{2,1,0:T(8,128)(2,1)}, u32[]{:S(2)}) copy-start(bf16[16,512,128]{2,1,0:T(8,128)(2,1)} %refs_3_.1) | copy-start | bytes 6291460
  50.5 27.5 %copy-start.1 = (f32[520,512]{1,0:T(8,128)S(1)}, f32[520,512]{1,0:T(8,128)}, u32[]{:S(2)}) copy-start(f32[520,512]{1,0:T(8,128)} %get-tuple-element.16.refs_0_) | copy-start | bytes 3194884
  50.5 27.5 %copy-start.2 = (bf16[32,2048]{1,0:T(8,128)(2,1)S(1)}, bf16[32,2048]{1,0:T(8,128)(2,1)}, u32[]{:S(2)}) copy-start(bf16[32,2048]{1,0:T(8,128)(2,1)} %hid_ref.3) | copy-start | bytes 393220
where the time goes:
time: 83.6 us; the launch traced here: 82.2 us
  Pallas kernels  76.1 us (91%)
  starting transfers between devices  3.31 us (4%)
  other arithmetic  1.43 us (2%)
  local copies, waits for them, and re-layouts  1.26 us (2%)
    pallas_call x1, Pallas kernels, prefix_parts(): pl.pallas_call(functools.partial(prefix_kernel, chips, scale2), out_shape...  44.5 us
    pallas_call x1, Pallas kernels, suffix_part(): pl.pallas_call(functools.partial(suffix_kernel, scale2, lat, heads, unrol...  27.4 us
    pallas_call x1, Pallas kernels, output_part(): pl.pallas_call(output_kernel, out_shape=jax.ShapeDtypeStruct(hidden.shape...  4.27 us
    ppermute x2, starting transfers between devices, send(): lax.ppermute(value, 'ctx', [(j, (j + hop * CORES) % group) for j in range...  3.31 us
  transfers between devices with their start and end apart: 2, of which 0 were waited for; matrix products, arithmetic and copies ran while one was open for 0% of the time, Pallas kernels for 33%

commit v1 on v0

--- a/solution.py
+++ b/solution.py
@@ -18,11 +18,24 @@
 NT = (((1,), (1,)), ((), ()))
 
 
-def rope_table(positions, half_dim):
-    lane = jnp.arange(4 * half_dim)
-    inv_freq = jnp.exp((lane % half_dim).astype(F32) * (-math.log(ROPE_BASE) / half_dim))
-    angle = positions.astype(F32)[:, None] * inv_freq
-    return jnp.where(lane < 2 * half_dim, jnp.cos(angle), jnp.sin(angle))
+TURN = (6.28125, 4059 / 2 ** 21, 2 * math.pi - 6.28125 - 4059 / 2 ** 21)
+
+
+def rope_rates(half_dim):
+    lane = jnp.arange(4 * half_dim) % half_dim
+    return jnp.exp(lane.astype(F32) * (-math.log(ROPE_BASE) / half_dim))[None, :]
+
+
+def rope_table(start, lens_ref, rate_ref, cs_ref):
+    rows, width = cs_ref.shape
+    for b in range(rows):
+        cs_ref[b:b + 1, :] = jnp.full((1, width), start + lens_ref[b], jnp.int32).astype(F32)
+    angle = cs_ref[...] * rate_ref[...]
+    turns = jnp.floor(angle * (0.5 / math.pi) + 0.5)
+    for part in TURN:
+        angle = angle - turns * part
+    lane = lax.broadcasted_iota(jnp.int32, (rows, width), 1)
+    cs_ref[...] = jnp.where(lane < width // 2, jnp.cos(angle), jnp.sin(angle))
 
 
 def prefix_part(scale2, lat, q_ref, k_ref, outs, work, hook=None, loaded=False, next_ref=None):
@@ -102,8 +115,8 @@
     x_ref[cut, :] = x_ref[cut, :] * c_x + y_ref[0:half, :] * c_y
 
 
-def prefix_kernel(chips, scale2, hid_ref, cs_ref, wq_hbm, wuk_hbm, kv_hbm, q_out, own_out, up_out, down_out,
-                  hid_all, cs_all, wq_buf, wuk_buf, k_ref, q_buf, res, far, got,
+def prefix_kernel(chips, scale2, start, lens_ref, hid_ref, rate_ref, wq_hbm, wuk_hbm, kv_hbm, q_out, own_out, up_out, down_out,
+                  hid_all, cs_ref, cs_all, wq_buf, wuk_buf, k_ref, q_buf, res, far, got,
                   s_ref, p_ref, acc_ref, a_ref, m_ref, l_ref,
                   wq_sem, wuk_sem, kv_sem, out_sem, hid_send, hid_recv, cs_send, cs_recv, kv_send, kv_recv, far_send, far_recv):
     me = lax.axis_index('ctx')
@@ -130,6 +143,7 @@
         weight_copy(i).start()
     own_copy = pltpu.make_async_copy(kv_hbm, k_ref.at[:, pl.ds(0, keys)], kv_sem)
     own_copy.start()
+    rope_table(start, lens_ref, rate_ref, cs_ref)
     partner = chip * CORES + (1 - core)
     peers = [((chip + chips - r) % chips) * CORES + core for r in range(1, chips)]
     barrier = pltpu.get_barrier_semaphore()
@@ -192,7 +206,7 @@
         c.wait()
 
 
-def prefix_parts(hidden, cs, w_q, w_uk, kv_prefix, scale2, chips):
+def prefix_parts(hidden, seq_lens, w_q, w_uk, kv_prefix, scale2, chips):
     rows, depth = hidden.shape
     heads, nope, lat = w_uk.shape
     rope = w_q.shape[1] // heads - nope
@@ -204,12 +218,12 @@
     full, half = (flat + 8, lat), (flat // 2 + 8, lat)
     dma = pltpu.SemaphoreType.DMA
     return pl.pallas_call(
-        functools.partial(prefix_kernel, chips, scale2),
+        functools.partial(prefix_kernel, chips, scale2, chips * keys),
         out_shape=[jax.ShapeDtypeStruct((flat, lat + rope), BF16)] + [jax.ShapeDtypeStruct(full, F32)] * 3,
-        in_specs=[VMEM, VMEM, HBM, HBM, HBM],
+        in_specs=[SMEM, VMEM, VMEM, HBM, HBM, HBM],
         out_specs=[HBM] * 4,
         scratch_shapes=[
-            pltpu.VMEM((others, rows, depth), BF16), pltpu.VMEM((others, rows, 2 * rope), F32),
+            pltpu.VMEM((others, rows, depth), BF16), pltpu.VMEM((rows, 2 * rope), F32), pltpu.VMEM((others, rows, 2 * rope), F32),
             pltpu.VMEM((steps, depth, wide), BF16), pltpu.VMEM(w_uk.shape, BF16),
             pltpu.VMEM((kv_prefix.shape[0], keys), BF16), pltpu.VMEM((chips, flat, lat + rope), BF16),
             pltpu.VMEM((3,) + full, F32), pltpu.VMEM((2,) + half, F32), pltpu.VMEM((2,) + half, F32),
@@ -219,7 +233,7 @@
         compiler_params=pltpu.CompilerParams(collective_id=0, has_side_effects=True, vmem_limit_bytes=60 * 2**20),
         cost_estimate=pl.CostEstimate(flops=2 * chips * flat * keys * (768 + lat), bytes_accessed=2 * w_q.size, transcendentals=chips * flat * keys),
         name='prefix',
-    )(hidden, cs, w_q, w_uk, kv_prefix)
+    )(seq_lens, hidden, rope_rates(rope // 2), w_q, w_uk, kv_prefix)
 
 
 def suffix_kernel(scale2, lat, heads, unroll, lens_ref, q_ref, kv_hbm, o_ref, m_out, l_out, q_buf, acc_ref, bufs, sems):
@@ -380,13 +394,10 @@
         rows = hidden.shape[0]
         heads, nope, lat = w_uk.shape
         head_w = w_q.shape[1] // heads
-        rope = head_w - nope
-        prefix_len = kv_prefix.shape[0] * group
         scale2 = head_w ** -0.5 * LOG2E
         kv_prefix = kv_prefix.T
         kv_suffix = kv_suffix.transpose(0, 2, 1)
-        cs = rope_table(prefix_len + seq_lens, rope // 2)
-        query, own, up, down = prefix_parts(hidden, cs, w_q, w_uk, kv_prefix, scale2, chips)
+        query, own, up, down = prefix_parts(hidden, seq_lens, w_q, w_uk, kv_prefix, scale2, chips)
 
         def send(value, hop):
             return lax.ppermute(value, 'ctx', [(j, (j + hop * CORES) % group) for j in range(group)])

time: 83.6 us -> 82 us (0.981)
  the two profiles are of different devices: /device:TPU:112 before, /device:TPU:113 now
where the time goes in v1:
time: 82 us; the launch traced here: 82.5 us
  Pallas kernels  77.9 us (95%)
  starting transfers between devices  2.75 us (3%)
  local copies, waits for them, and re-layouts  1.26 us (2%)
    pallas_call x1, Pallas kernels, prefix_parts(): pl.pallas_call(functools.partial(prefix_kernel, chips, scale2, chips * ke...  44.1 us
    pallas_call x1, Pallas kernels, suffix_part(): pl.pallas_call(functools.partial(suffix_kernel, scale2, lat, heads, unrol...  29.6 us
    pallas_call x1, Pallas kernels, output_part(): pl.pallas_call(output_kernel, out_shape=jax.ShapeDtypeStruct(hidden.shape...  4.27 us
    ppermute x2, starting transfers between devices, send(): lax.ppermute(value, 'ctx', [(j, (j + hop * CORES) % group) for j in range...  2.75 us
  transfers between devices with their start and end apart: 2, of which 0 were waited for; matrix products, arithmetic and copies ran while one was open for 0% of the time, Pallas kernels for 36%

profile of v1, /device:TPU:113, one launch (start us, length us, event | category | flops | bytes accessed | tf_op | source)
XLA Modules:
  0.0 82.5 jit_solution(8973821364170307386)
XLA Ops:
  0.0 0.5 fusion.2.rate_ref
  0.5 0.0 copy-start.3
  0.5 44.1 %prefix.1 = (bf16[512,576]{1,0:T(8,128)(2,1)}, f32[520,512]{1,0:T(8,128)}, f32[520,512]{1,0:T(8,128)}, f32[520,512]{1,0:T(8,128)}) custom-call(s32[32]{0:T(128)} %lens_ref.3, bf16[32,2048]{1,0:T(8,128)(2,1)} %hid_ref.3, f32[1,128]{1,0:T(1,128)} %fusion.2.rate_ref, bf16[2048,3072]{1,0:T(8,128)(2,1)} %wq_hbm.1, bf16[16,128,512]{2,1,0:T(8,128)(2,1)} %wuk_hbm.1, ...), custom_call_target="tpu_custom_call" | custom-call | flops 21474836480 | bytes 12582912 | tf_op jit(solution)/shard_map/prefix/pallas_call | solution.py:220
  44.6 0.1 collective-permute-start
  44.7 2.7 %collective-permute-start.1 = (f32[520,512]{1,0:T(8,128)}, f32[520,512]{1,0:T(8,128)S(1)}, u32[]{:S(2)}, u32[]{:S(2)}) collective-permute-start(f32[520,512]{1,0:T(8,128)} %get-tuple-element.18), channel_id=1, source_target_pairs={{0,6},{1,7},{2,0},{3,1},{4,2},{5,3},{6,4},{7,5},{8,14},{9,15},{10,... | collective-permute-start | bytes 3194888 | tf_op jit(solution)/shard_map/ppermute | solution.py:403
  47.3 0.0 slice-start
  47.4 0.0 copy-done.3
  47.4 0.0 copy-start.4
  47.4 1.2 %copy-done.4 = bf16[512,576]{1,0:T(8,128)(2,1)S(1)} copy-done((bf16[512,576]{1,0:T(8,128)(2,1)S(1)}, bf16[512,576]{1,0:T(8,128)(2,1)}, u32[]{:S(2)}) %copy-start.4) | copy-done | bytes 589848
  48.6 0.0 slice-start.1
  48.6 0.0 copy-start
  48.6 0.0 copy-start.1
  48.6 0.0 copy-start.2
  48.6 29.6 %suffix.1 = (f32[4,512,128]{2,1,0:T(8,128)S(1)}, f32[512,128]{1,0:T(8,128)S(1)}, f32[512,128]{1,0:T(8,128)S(1)}) custom-call(s32[32]{0:T(128)S(1)} %copy-done.3, bf16[512,576]{1,0:T(8,128)(2,1)S(1)} %copy-done.4, bf16[32,576,2048]{2,1,0:T(8,128)(2,1)} %bitcast.1.kv_hbm), custom_call_target="tpu_custom_call" | custom-call | flops 25769803776 | bytes 75497472 | tf_op jit(solution)/shard_map/suffix/pallas_call | solution.py:331
  78.2 0.0 collective-permute-done.refs_1_
  78.2 0.0 collective-permute-done.1.refs_2_
  78.2 0.0 slice-done
  78.2 0.0 slice-done.1
  78.2 0.0 copy-done
  78.2 0.0 copy-done.1
  78.2 0.0 copy-done.2
  78.3 4.3 %output.1 = bf16[32,2048]{1,0:T(8,128)(2,1)} custom-call(bf16[32,2048]{1,0:T(8,128)(2,1)S(1)} %copy-done.2, f32[4,512,128]{2,1,0:T(8,128)S(1)} %get-tuple-element.13.os_ref, f32[512,128]{1,0:T(8,128)S(1)} %get-tuple-element.14.ms_ref, f32[512,128]{1,0:T(8,128)S(1)} %get-tuple-element.15.ls_ref, f32[520,512]{1,0:T(8,128)S(1)} %copy-done.1, ...), custom_call_target="tpu_custom_call" | custom-call | flops 335544320 | bytes 10485760 | tf_op jit(solution)/shard_map/output/pallas_call | solution.py:375
  (1 shorter events, 0.0 us)
Async XLA Ops:
  0.5 46.8 %copy-start.3 = (s32[32]{0:T(128)S(1)}, s32[32]{0:T(128)}, u32[]{:S(2)}) copy-start(s32[32]{0:T(128)} %lens_ref.3) | copy-start | bytes 388
  44.6 33.6 %collective-permute-start = (f32[520,512]{1,0:T(8,128)}, f32[520,512]{1,0:T(8,128)S(1)}, u32[]{:S(2)}, u32[]{:S(2)}) collective-permute-start(f32[520,512]{1,0:T(8,128)} %get-tuple-element.17), channel_id=1, source_target_pairs={{0,2},{1,3},{2,4},{3,5},{4,6},{5,7},{6,0},{7,1},{8,10},{9,11},{10,... | collective-permute-start | bytes 3194888 | tf_op jit(solution)/shard_map/ppermute | solution.py:403
  44.7 33.5 %collective-permute-start.1 = (f32[520,512]{1,0:T(8,128)}, f32[520,512]{1,0:T(8,128)S(1)}, u32[]{:S(2)}, u32[]{:S(2)}) collective-permute-start(f32[520,512]{1,0:T(8,128)} %get-tuple-element.18), channel_id=1, source_target_pairs={{0,6},{1,7},{2,0},{3,1},{4,2},{5,3},{6,4},{7,5},{8,14},{9,15},{10,... | collective-permute-start | bytes 3194888 | tf_op jit(solution)/shard_map/ppermute | solution.py:403
  47.3 30.9 %slice-start = ((s8[8388608]{0:T(1024)(128)(4,1)}), s8[4194304]{0:T(1024)(128)(4,1)S(1)}, s32[]{:S(2)}) async-start(s8[8388608]{0:T(1024)(128)(4,1)} %bitcast.2), calls=%async_computation | async-start | bytes 8388608
  47.4 1.2 %copy-start.4 = (bf16[512,576]{1,0:T(8,128)(2,1)S(1)}, bf16[512,576]{1,0:T(8,128)(2,1)}, u32[]{:S(2)}) copy-start(bf16[512,576]{1,0:T(8,128)(2,1)} %get-tuple-element.12.q_ref) | copy-start | bytes 1769476
  48.6 29.6 %slice-start.1 = ((s8[8388608]{0:T(1024)(128)(4,1)}), s8[4194304]{0:T(1024)(128)(4,1)S(1)}, s32[]{:S(2)}) async-start(s8[8388608]{0:T(1024)(128)(4,1)} %bitcast.2), calls=%async_computation.1 | async-start | bytes 8388608
  48.6 29.6 %copy-start = (bf16[16,512,128]{2,1,0:T(8,128)(2,1)S(1)}, bf16[16,512,128]{2,1,0:T(8,128)(2,1)}, u32[]{:S(2)}) copy-start(bf16[16,512,128]{2,1,0:T(8,128)(2,1)} %refs_3_.1) | copy-start | bytes 6291460
  48.6 29.6 %copy-start.1 = (f32[520,512]{1,0:T(8,128)S(1)}, f32[520,512]{1,0:T(8,128)}, u32[]{:S(2)}) copy-start(f32[520,512]{1,0:T(8,128)} %get-tuple-element.16.refs_0_) | copy-start | bytes 3194884
  48.6 29.6 %copy-start.2 = (bf16[32,2048]{1,0:T(8,128)(2,1)S(1)}, bf16[32,2048]{1,0:T(8,128)(2,1)}, u32[]{:S(2)}) copy-start(bf16[32,2048]{1,0:T(8,128)(2,1)} %hid_ref.3) | copy-start | bytes 393220
